TPU v7x, 256 devices: a 8x8x2 block of a 8x8x16 slice. The times are simulated.
256 devices in a mesh: member: 2 (over z), band: 128 (over x, y, core).
Axes of the slice: x: 8, y: 8, z: 2, core: 2. Of those that a mesh axis runs over, the one named last changes fastest.
The devices are a block of a 8x8x16 slice.
Arguments:
- grid_in: bfloat16 [256, 274, 5248], P(('member', 'band')), parts along dimension 0, may hold values from -6 to 6
- legendre: bfloat16 [128, 2, 640, 64], P('band'), may hold values from -0.75 to 0.75
- gauss_weight: float32 [64], replicated, may hold values from 0.2 to 2
- vertical_modes: float32 [137, 137], replicated
- coupling: float32 [137, 137], replicated, may hold values from -0.5 to 0.5
- mode_rates: float32 [137], replicated, may hold values from 0.1 to 10
- loop_length: int32 [128], replicated, may hold values from 20 to 5136, as said below
- lat_order: int32 [128], replicated, may hold values from 0 to 127, each once
- wave_number: int32 [128], replicated, may hold values from 0 to 1279, as said below
Outputs:
- grid_out: bfloat16 [256, 274, 5248], P(('member', 'band')), parts along dimension 0
There are 2 independent parts, one for each index of `member`. A program takes and returns all parts, laid end to end along the dimension named above; an argument that names none is the same for every part. Nothing has to cross between parts.
Inputs may be any that keep to these rules, and one draw needn't show every extreme that they name: loop_length[t] = 20 + 4 k with k not falling from the poles toward the equator, equal for latitudes t and 127 - t; the equatorial loops have 5248 - 112 points. Row i of grid_in and grid_out holds latitude lat_order[i]. `wave_number`: distinct values.
All inputs are finite; a program needn't handle non-finite values.
Results may differ from a plain program's by a relative error of at most 0.013.
Values may be sent and summed in bfloat16 or wider, within the bound.
A program may use at most 64 MiB of HBM per device.

v0:
```python
import math

import jax
import jax.numpy as jnp
from jax import lax
from jax.sharding import Mesh
from jax.sharding import PartitionSpec as P

TRUNC = 1279
BAND = ("band_0", "band_1", "band_2")
MEMBER_BAND = ("member", "band_0", "band_1", "band_2")


implicit_step = 0.5


def in_blocks(shard, dim, length):
    dims = shard.shape
    tiles = shard.reshape(*dims[:dim], length, dims[dim] // length, *dims[dim + 1 :])
    return jnp.moveaxis(tiles, dim, 0)


def laid_out(tiles, dim):
    tiles = jnp.moveaxis(tiles, 0, dim)
    dims = tiles.shape
    return tiles.reshape(*dims[:dim], dims[dim] * dims[dim + 1], *dims[dim + 2 :])


def exchange_in_order(tiles, axes, turns):
    inside = tiles.shape[1:]
    filled = tiles.reshape(*(lax.axis_size(a) for a in axes), *inside)
    for k in turns:
        filled = lax.all_to_all(filled, axes[k], k, k, tiled=True)
    return filled.reshape(-1, *inside)


def two_step_exchange(shard, groups, turns, split_dim, concat_dim):
    length = lax.axis_size(groups[0]) * lax.axis_size(groups[1])
    tiles = in_blocks(shard, split_dim, length)
    return laid_out(exchange_in_order(tiles, groups, turns), concat_dim)


def loop_tables(length, wave_list, block_count):
    offsets = jnp.arange(128, dtype=jnp.int32)
    inner_turn = offsets[:, None] * wave_list[None, :] % length
    angles = inner_turn.astype(jnp.float32) * (2.0 * math.pi) / length.astype(jnp.float32)
    inner_table = jnp.concatenate([jnp.cos(angles), jnp.sin(angles)], axis=1).astype(jnp.bfloat16)
    block_index = jnp.arange(block_count, dtype=jnp.int32)
    outer_turn = block_index[:, None] * 128 * wave_list[None, :] % length
    phases = outer_turn.astype(jnp.float32) * (2.0 * math.pi) / length.astype(jnp.float32)
    return (inner_table, jnp.cos(phases), jnp.sin(phases))


def forward_loop(one_loop, length, wave_list):
    field_count, loop_width = one_loop.shape
    block_count = loop_width // 128
    wave_count = wave_list.shape[0]
    inner_table, cos_turn, sin_turn = loop_tables(length, wave_list, block_count)
    inside = jnp.arange(loop_width, dtype=jnp.int32) < length
    masked = jnp.where(inside[None, :], one_loop, jnp.zeros((), one_loop.dtype))
    products = jnp.dot(
        masked.reshape(field_count * block_count, 128),
        inner_table,
        preferred_element_type=jnp.float32,
    )
    products = products.reshape(field_count, block_count, 2, wave_count)
    real_part = jnp.sum(cos_turn * products[:, :, 0] - sin_turn * products[:, :, 1], axis=1)
    imag_part = -jnp.sum(sin_turn * products[:, :, 0] + cos_turn * products[:, :, 1], axis=1)
    inverse_len = 1.0 / length.astype(jnp.float32)
    together = jnp.concatenate([real_part, imag_part], axis=0) * inverse_len
    resolved = 2 * wave_list < length
    together = jnp.where(resolved[None, :], together, 0.0)
    return together.T.astype(jnp.bfloat16)


def inverse_loop(fourier, length, wave_list, loop_width):
    block_count = loop_width // 128
    wave_count = wave_list.shape[0]
    field_count = fourier.shape[1] // 2
    inner_table, cos_turn, sin_turn = loop_tables(length, wave_list, block_count)
    doubling = jnp.where(wave_list == 0, 1.0, 2.0).astype(jnp.float32)
    real_part = fourier[:, :field_count].astype(jnp.float32).T * doubling
    imag_part = fourier[:, field_count:].astype(jnp.float32).T * doubling
    cosine_part = real_part[:, None, :] * cos_turn[None] - imag_part[:, None, :] * sin_turn[None]
    sine_part = -(real_part[:, None, :] * sin_turn[None] + imag_part[:, None, :] * cos_turn[None])
    combined = jnp.concatenate([cosine_part, sine_part], axis=2).astype(jnp.bfloat16)
    points = lax.dot_general(
        combined.reshape(field_count * block_count, 2 * wave_count),
        inner_table,
        (((1,), (1,)), ((), ())),
        preferred_element_type=jnp.float32,
    )
    points = points.reshape(field_count, loop_width)
    inside = jnp.arange(loop_width, dtype=jnp.int32) < length
    return jnp.where(inside[None, :], points, 0.0).astype(jnp.bfloat16)


def semi_implicit(spectral, wave_values, vertical_modes, coupling, mode_rates):
    half_rows = spectral.shape[-2]
    level_count = vertical_modes.shape[0]
    parity = jnp.arange(2, dtype=jnp.int32)
    row_index = jnp.arange(half_rows, dtype=jnp.int32)
    degree = wave_values[..., None, None] + parity[:, None] + 2 * row_index[None, :]
    kept_rows = degree <= TRUNC
    spectral = jnp.where(kept_rows[..., None], spectral, 0.0)
    damping = (degree * (degree + 1)).astype(jnp.float32) / float(TRUNC * (TRUNC + 1))
    reshaped = spectral.reshape(spectral.shape[:-1] + (2, 2, level_count))
    divergence = reshaped[..., 0, :]
    pressure = reshaped[..., 1, :]
    factor_e = damping[..., None, None]
    right_side = divergence - implicit_step * factor_e * jnp.einsum(
        "...l,kl->...k", pressure, coupling
    )
    in_modes = jnp.einsum("...l,lk->...k", right_side, vertical_modes)
    in_modes = in_modes / (1.0 + implicit_step * factor_e * mode_rates)
    new_div = jnp.einsum("...k,lk->...l", in_modes, vertical_modes)
    new_press = pressure - implicit_step * jnp.einsum("...l,kl->...k", new_div, coupling)
    updated = jnp.stack([new_div, new_press], axis=-2)
    return updated.reshape(spectral.shape).astype(jnp.bfloat16)


def per_device(
    grid_in,
    legendre,
    gauss_weight,
    vertical_modes,
    coupling,
    mode_rates,
    loop_length,
    lat_order,
    wave_number,
):
    groups = lax.axis_size(BAND)
    band_index = lax.axis_index(BAND)
    loop_count, field_count, loop_width = grid_in.shape
    slot_count = legendre.shape[0]
    lat_count = lat_order.shape[0]
    half_count = lat_count // 2
    column_count = 2 * field_count
    wave_total = wave_number.shape[0]
    own_rows = lax.dynamic_slice_in_dim(lat_order, band_index * loop_count, loop_count)
    own_lengths = jnp.take(loop_length, own_rows)
    column_waves = wave_number.reshape(groups, slot_count).T.reshape(wave_total)
    own_waves = lax.dynamic_slice_in_dim(wave_number, band_index * slot_count, slot_count)

    def forward_piece(scan_carry, scan_item):
        one_loop, length = scan_item
        loop_piece = forward_loop(one_loop, length, column_waves).reshape(
            slot_count, groups, column_count
        )
        return (
            scan_carry,
            two_step_exchange(loop_piece, (("band_0", "band_1"), "band_2"), (0, 1), 1, 1),
        )

    unused, pieces = lax.scan(forward_piece, 0, (grid_in, own_lengths))
    arrived = jnp.transpose(pieces, (1, 2, 0, 3))
    arrived = arrived.reshape(slot_count, lat_count, column_count)
    row_of_lat = jnp.argsort(lat_order)
    northern = jnp.take(arrived, row_of_lat[:half_count], axis=1).astype(jnp.float32)
    southern = jnp.take(arrived, row_of_lat[::-1][:half_count], axis=1).astype(jnp.float32)
    weight = gauss_weight[None, :, None]
    even_part = (weight * (northern + southern)).astype(jnp.bfloat16)
    odd_part = (weight * (northern - southern)).astype(jnp.bfloat16)
    stacked = jnp.stack([even_part, odd_part], axis=1)
    spectral = jnp.einsum("kprj,kpjc->kprc", legendre, stacked, preferred_element_type=jnp.float32)
    updated = semi_implicit(spectral, own_waves, vertical_modes, coupling, mode_rates)
    summed = jnp.einsum("kprj,kprc->kpjc", legendre, updated, preferred_element_type=jnp.float32)
    northern_back = summed[:, 0] + summed[:, 1]
    southern_back = summed[:, 0] - summed[:, 1]
    by_lat = jnp.concatenate([northern_back, southern_back[:, ::-1]], axis=1)
    resolved = 2 * own_waves[:, None] < loop_length[None, :]
    by_lat = jnp.where(resolved[:, :, None], by_lat, 0.0).astype(jnp.bfloat16)
    returning = jnp.take(by_lat, lat_order, axis=1).reshape(
        slot_count, groups, loop_count, column_count
    )
    outgoing_loops = jnp.transpose(returning, (2, 0, 1, 3))

    def inverse_piece(scan_carry, scan_item):
        loop_data, length = scan_item
        loop_back = two_step_exchange(loop_data, (("band_0", "band_1"), "band_2"), (1, 0), 1, 1)
        return (
            scan_carry,
            inverse_loop(
                loop_back.reshape(wave_total, column_count), length, column_waves, loop_width
            ),
        )

    unused, grid_out = lax.scan(inverse_piece, 0, (outgoing_loops, own_lengths))
    return grid_out


def solution(mesh):
    torus = Mesh(
        mesh.devices.reshape(mesh.shape["member"], 8, 8, 2),
        ("member", "band_0", "band_1", "band_2"),
    )
    in_specs = (
        P(MEMBER_BAND, None, None),
        P(BAND, None, None, None),
        P(),
        P(),
        P(),
        P(),
        P(),
        P(),
        P(),
    )
    out_specs = P(MEMBER_BAND, None, None)
    return jax.shard_map(
        per_device, mesh=torus, in_specs=in_specs, out_specs=out_specs, check_vma=False
    )
```

profile of v0, /device:TPU:513, one launch (start us, length us, event | category | flops | bytes accessed | tf_op | source)
XLA Modules:
  0.0 123.4 jit_solution(9092805814212016353)
XLA Ops:
  0.0 1.3 %dynamic_slice.17 = s32[1]{0:T(128)} dynamic-slice(s32[128]{0:T(128)} %param.18, s32[]{:T(128)S(6)} %select_n.130), dynamic_slice_sizes={1} | dynamic-slice | bytes 12 | tf_op jit(solution)/shard_map/dynamic_slice | solution.py:141
  3.2 1.2 %dynamic-slice.3 = s32[1]{0:T(128)} dynamic-slice(s32[128]{0:T(128)} %param.17, s32[]{:T(128)} %bitcast), dynamic_slice_sizes={1} | dynamic-slice | bytes 12 | tf_op jit(solution)/shard_map/jit(_take)/gather | solution.py:142
  5.6 3.7 %broadcast_select_fusion = bf16[1,274,5248]{2,1,0:T(8,128)(2,1)} fusion(bf16[1,274,5248]{2,1,0:T(8,128)(2,1)} %param.11, pred[5248]{0:T(1024)(128)(4,1)S(1)} %iota_compare_fusion), kind=kLoop, calls=%fused_computation.16 | loop fusion | flops 1437952 | bytes 5757056 | tf_op jit(solution)/shard_map/while/body/eval_jaxpr/jit(_where)/select_n | solution.py:60
  9.3 4.2 %select_n.137 = bf16[274,41,128]{2,1,0:T(8,128)(2,1)S(1)} reshape(bf16[1,274,5248]{2,1,0:T(8,128)(2,1)} %broadcast_select_fusion) | data formatting | bytes 5751808 | tf_op jit(solution)/shard_map/while/body/eval_jaxpr/jit(_where)/select_n | solution.py:60
  14.0 1.0 cosine_convert_fusion
  15.0 1.1 fusion.57
  16.2 1.7 %fusion.4 = f32[274,41,2,128]{3,0,2,1:T(8,128)S(1)} fusion(bf16[2,128,128,1]{2,1,0,3:T(8,128)(2,1)S(1)} %bitcast.140, bf16[274,41,128,1]{2,1,0,3:T(8,128)(2,1)S(1)} %bitcast.136), kind=kOutput, calls=%fused_computation.14 | convolution fusion | flops 736231424 | bytes 14445056 | tf_op jit(solution)/shard_map/while/body/eval_jaxpr/dot_general | solution.py:61
  18.0 1.9 %subtract_reduce_fusion = (f32[274,128]{1,0:T(8,128)S(1)}, f32[274,128]{1,0:T(8,128)S(1)}) fusion(f32[274,41,2,128]{3,0,2,1:T(8,128)S(1)} %fusion.4, f32[41,128]{1,0:T(8,128)S(1)} %get-tuple-element.64, f32[41,128]{1,0:T(8,128)S(1)} %get-tuple-element.63), kind=kLoop, calls=%fused_computation.9 | loop fusion | flops 11433472 | bytes 11826176 | tf_op jit(solution)/shard_map/while/body/eval_jaxpr/reduce_sum | solution.py:67
  20.2 0.7 reshape.467
  21.0 21.8 %all-to-all-start = ((bf16[64,2,1,1,548]{4,1,3,2,0:T(2,128)(2,1)}), bf16[64,2,1,1,548]{4,1,3,2,0:T(2,128)(2,1)S(1)}, u32[]{:S(2)}, u32[]{:S(2)}) async-start(bf16[64,2,1,1,548]{4,1,3,2,0:T(2,128)(2,1)} %bitcast.11), calls=%async_computation | async-start | bytes 327680 | tf_op jit(solution)/shard_map/while/body/eval_jaxpr/all_to_all | solution.py:33
  42.8 2.6 %sort.17 = (s32[128]{0:T(128)}, s32[128]{0:T(128)S(1)}) sort(s32[128]{0:T(128)S(1)} %copy-done.17, s32[128]{0:T(128)S(1)} %iota.42), dimensions={0}, to_apply=%region_2.3 | sort | flops 896 | bytes 2048 | tf_op jit(solution)/shard_map/jit(argsort)/sort | solution.py:159
  48.1 1.0 multiply_add_fusion
  49.1 4.2 %all-to-all-done = bf16[64,2,1,1,548]{4,1,3,2,0:T(2,128)(2,1)S(1)} async-done(((bf16[64,2,1,1,548]{4,1,3,2,0:T(2,128)(2,1)}), bf16[64,2,1,1,548]{4,1,3,2,0:T(2,128)(2,1)S(1)}, u32[]{:S(2)}, u32[]{:S(2)}) %all-to-all-start) | async-done | bytes 140320 | tf_op jit(solution)/shard_map/while/body/eval_jaxpr/all_to_all | solution.py:33
  53.3 9.8 %all_to_all.24 = bf16[64,2,1,1,548]{4,0,3,2,1:T(8,128)(2,1)S(1)} all-to-all(bf16[64,2,1,1,548]{4,0,3,2,1:T(8,128)(2,1)S(1)} %copy.28), channel_id=1, replica_groups=mesh['member'=2,'band_0'=8,'band_1'=8,'band_2'=2] {'band_2'}, dimensions={1} | all-to-all | bytes 280576 | tf_op jit(solution)/shard_map/while/body/eval_jaxpr/all_to_all | solution.py:33
  63.4 0.7 gather_fusion.2
  65.6 1.4 %copy.30 = f32[2,640,548]{1,0,2:T(2,128)S(1)} copy(f32[2,640,548]{1,2,0:T(8,128)S(1)} %select_bitcast_fusion) | data formatting | bytes 5611520 | tf_op jit(solution)/shard_map/jit(_where)/select_n | solution.py:105
  67.1 1.0 fusion.67
  68.1 1.7 %fusion.7 = f32[2,640,2,137]{1,3,2,0:T(8,128)} fusion(f32[1,2,640,2,1,137]{2,1,5,4,3,0:T(2,128)S(1)} %get-tuple-element.54, f32[1,2,640,2,1,137]{2,1,5,4,3,0:T(2,128)S(1)} %get-tuple-element.53, f32[2,640]{1,0:T(2,128)S(1)} %fusion.59, f32[137,137]{1,0:T(8,128)S(1)} %copy-done.2, f32[137,137]{1,0:T(8,128)S(1)} %copy-done.5), kind=kOutput, calls=%fused_computation.22 | convolution fusion | flops 193246720 | bytes 4363912 | tf_op jit(solution)/shard_map/...l,lk->...k/dot_general | solution.py:114
  69.7 1.9 %fusion.9 = bf16[2,640,2,137]{1,3,2,0:T(8,128)(2,1)S(1)} fusion(f32[2,640,2,137]{1,3,2,0:T(8,128)} %fusion.7, f32[2,640,137]{1,2,0:T(8,128)} %multiply_add_fusion, f32[137,137]{1,0:T(8,128)S(1)} %copy-done.5), kind=kOutput, calls=%fused_computation.24 | convolution fusion | flops 96448000 | bytes 2880836 | tf_op jit(solution)/shard_map/...k,lk->...l/dot_general | solution.py:116
  72.2 1.1 copy.34
  74.2 0.9 gather_fusion
  75.4 3.8 %all_to_all.25 = bf16[64,2,1,1,548]{4,0,3,2,1:T(8,128)(2,1)S(1)} all-to-all(bf16[64,2,1,1,548]{4,0,3,2,1:T(8,128)(2,1)S(1)} %copy.36), channel_id=1, replica_groups=mesh['member'=2,'band_0'=8,'band_1'=8,'band_2'=2] {'band_2'}, dimensions={1} | all-to-all | bytes 280576 | tf_op jit(solution)/shard_map/while/body/eval_jaxpr/all_to_all | solution.py:33
  79.2 0.8 copy.37
  80.1 8.3 %all-to-all-start.3 = ((bf16[64,2,1,1,548]{4,1,3,2,0:T(2,128)(2,1)}), bf16[64,2,1,1,548]{4,1,3,2,0:T(2,128)(2,1)S(1)}, u32[]{:S(2)}, u32[]{:S(2)}) async-start(bf16[64,2,1,1,548]{4,1,3,2,0:T(2,128)(2,1)} %copy.37), calls=%async_computation.3 | async-start | bytes 327680 | tf_op jit(solution)/shard_map/while/body/eval_jaxpr/all_to_all | solution.py:33
  88.4 10.1 %all-to-all-done.3 = bf16[64,2,1,1,548]{4,1,3,2,0:T(2,128)(2,1)S(1)} async-done(((bf16[64,2,1,1,548]{4,1,3,2,0:T(2,128)(2,1)}), bf16[64,2,1,1,548]{4,1,3,2,0:T(2,128)(2,1)S(1)}, u32[]{:S(2)}, u32[]{:S(2)}) %all-to-all-start.3) | async-done | bytes 140320 | tf_op jit(solution)/shard_map/while/body/eval_jaxpr/all_to_all | solution.py:33
  99.0 3.4 %subtract_convert_fusion = (bf16[274,41,128]{2,0,1:T(8,128)(2,1)}, bf16[274,41,128]{2,0,1:T(8,128)(2,1)S(1)}) fusion(f32[274,128]{1,0:T(8,128)S(1)} %copy.39, f32[274,128]{1,0:T(8,128)S(1)} %copy.38, f32[41,128]{1,0:T(8,128)S(1)} %copy-done.4, f32[41,128]{1,0:T(8,128)S(1)} %get-tuple-element.63), kind=kLoop, calls=%fused_computation.7 | loop fusion | flops 12941568 | bytes 6074368 | tf_op jit(solution)/shard_map/convert.3
  102.9 2.5 %neg.14 = bf16[11234,128]{1,0:T(8,128)(2,1)} reshape(bf16[274,41,128]{2,1,0:T(8,128)(2,1)S(1)} %copy.41) | data formatting | bytes 5751808 | tf_op jit(solution)/shard_map/while/body/eval_jaxpr/neg | solution.py:85
  105.4 2.3 %copy.40 = bf16[274,41,128]{2,1,0:T(8,128)(2,1)S(1)} copy(bf16[274,41,128]{2,0,1:T(8,128)(2,1)} %get-tuple-element.55) | data formatting | bytes 5751808 | tf_op jit(solution)/shard_map/convert.3
  107.7 2.5 %sub.44 = bf16[11234,128]{1,0:T(8,128)(2,1)} reshape(bf16[274,41,128]{2,1,0:T(8,128)(2,1)S(1)} %copy.40) | data formatting | bytes 5751808 | tf_op jit(solution)/shard_map/while/body/eval_jaxpr/sub | solution.py:84
  110.2 6.0 %fusion = bf16[11234,128]{1,0:T(8,128)(2,1)} fusion(bf16[11234,128]{1,0:T(8,128)(2,1)} %neg.14, bf16[11234,128]{1,0:T(8,128)(2,1)} %sub.44, bf16[128,128]{0,1:T(8,128)(2,1)S(1)} %copy-done.9, bf16[128,128]{0,1:T(8,128)(2,1)S(1)} %copy-done.7), kind=kOutput, calls=%fused_computation.10 | convolution fusion | flops 747866112 | bytes 8693248 | tf_op jit(solution)/shard_map/while/body/eval_jaxpr/dot_general | solution.py:87
  116.1 5.2 %reshape.473 = bf16[1,274,5248]{2,1,0:T(8,128)(2,1)S(1)} reshape(bf16[11234,128]{1,0:T(8,128)(2,1)} %fusion) | data formatting | bytes 5751808 | tf_op jit(solution)/shard_map/while/body/eval_jaxpr/reshape | solution.py:93
  121.3 2.1 %select_convert_fusion = bf16[1,274,5248]{2,1,0:T(8,128)(2,1)} fusion(bf16[1,274,5248]{2,1,0:T(8,128)(2,1)S(1)} %reshape.473, pred[5248]{0:T(1024)(128)(4,1)S(1)} %copy-done.11), kind=kLoop, calls=%fused_computation.5 | loop fusion | flops 1437952 | bytes 5757056 | tf_op jit(solution)/shard_map/while/body/eval_jaxpr/convert_element_type | solution.py:95
  (84 shorter events, 7.7 us)
Async XLA Ops:
  0.0 65.0 %copy-start = (bf16[1,2,640,64]{2,3,1,0:T(8,128)(2,1)S(1)}, bf16[1,2,640,64]{2,3,1,0:T(8,128)(2,1)}, u32[]{:S(2)}) copy-start(bf16[1,2,640,64]{2,3,1,0:T(8,128)(2,1)} %param.12) | copy-start | bytes 491524
  5.1 0.6 copy-start.10
  9.3 4.2 %copy-start.12 = (s32[128]{0:T(128)S(1)}, s32[128]{0:T(128)}, u32[]{:S(2)}) copy-start(s32[128]{0:T(128)} %param.19) | copy-start | bytes 1540
  15.0 2.9 %copy-start.6 = (bf16[128,128]{0,1:T(8,128)(2,1)}, bf16[128,128]{0,1:T(8,128)(2,1)S(1)}, u32[]{:S(2)}) copy-start(bf16[128,128]{0,1:T(8,128)(2,1)S(1)} %get-tuple-element.65) | copy-start | bytes 98308
  15.0 2.9 %copy-start.8 = (bf16[128,128]{0,1:T(8,128)(2,1)}, bf16[128,128]{0,1:T(8,128)(2,1)S(1)}, u32[]{:S(2)}) copy-start(bf16[128,128]{0,1:T(8,128)(2,1)S(1)} %get-tuple-element.66) | copy-start | bytes 98308
  16.1 1.8 %copy-start.3 = (f32[41,128]{1,0:T(8,128)}, f32[41,128]{1,0:T(8,128)S(1)}, u32[]{:S(2)}) copy-start(f32[41,128]{1,0:T(8,128)S(1)} %get-tuple-element.64) | copy-start | bytes 62980
  17.9 2.1 %copy-start.16 = (pred[128]{0:T(512)(128)(4,1)S(1)}, pred[128]{0:T(512)(128)(4,1)}, u32[]{:S(2)}) copy-start(pred[128]{0:T(512)(128)(4,1)} %multiply_compare_fusion) | copy-start | bytes 388
  17.9 24.9 %copy-start.17 = (s32[128]{0:T(128)S(1)}, s32[128]{0:T(128)}, u32[]{:S(2)}) copy-start(s32[128]{0:T(128)} %param.18) | copy-start | bytes 1540
  18.0 27.7 %copy-start.13 = (s32[128]{0:T(128)S(1)}, s32[128]{0:T(128)}, u32[]{:S(2)}) copy-start(s32[128]{0:T(128)} %param.19) | copy-start | bytes 1540
  18.0 29.9 %copy-start.18 = (s32[128]{0:T(128)S(1)}, s32[128]{0:T(128)}, u32[]{:S(2)}) copy-start(s32[128]{0:T(128)} %param.17) | copy-start | bytes 1540
  18.0 30.1 %copy-start.14 = (f32[137]{0:T(256)S(1)}, f32[137]{0:T(256)}, u32[]{:S(2)}) copy-start(f32[137]{0:T(256)} %param.16) | copy-start | bytes 1648
  19.9 44.9 %copy-start.15 = (f32[64]{0:T(128)S(1)}, f32[64]{0:T(128)}, u32[]{:S(2)}) copy-start(f32[64]{0:T(128)} %param.13) | copy-start | bytes 772
  21.0 32.3 %all-to-all-start = ((bf16[64,2,1,1,548]{4,1,3,2,0:T(2,128)(2,1)}), bf16[64,2,1,1,548]{4,1,3,2,0:T(2,128)(2,1)S(1)}, u32[]{:S(2)}, u32[]{:S(2)}) async-start(bf16[64,2,1,1,548]{4,1,3,2,0:T(2,128)(2,1)} %bitcast.11), calls=%async_computation | async-start | bytes 327680 | tf_op jit(solution)/shard_map/while/body/eval_jaxpr/all_to_all | solution.py:33
  67.1 1.0 copy-start.2
  67.1 1.0 copy-start.5
  73.9 25.1 %copy-start.4 = (f32[41,128]{1,0:T(8,128)S(1)}, f32[41,128]{1,0:T(8,128)}, u32[]{:S(2)}) copy-start(f32[41,128]{1,0:T(8,128)} %copy-done.3) | copy-start | bytes 62980
  80.1 18.5 %all-to-all-start.3 = ((bf16[64,2,1,1,548]{4,1,3,2,0:T(2,128)(2,1)}), bf16[64,2,1,1,548]{4,1,3,2,0:T(2,128)(2,1)S(1)}, u32[]{:S(2)}, u32[]{:S(2)}) async-start(bf16[64,2,1,1,548]{4,1,3,2,0:T(2,128)(2,1)} %copy.37), calls=%async_computation.3 | async-start | bytes 327680 | tf_op jit(solution)/shard_map/while/body/eval_jaxpr/all_to_all | solution.py:33
  107.7 2.5 %copy-start.7 = (bf16[128,128]{0,1:T(8,128)(2,1)S(1)}, bf16[128,128]{0,1:T(8,128)(2,1)}, u32[]{:S(2)}) copy-start(bf16[128,128]{0,1:T(8,128)(2,1)} %copy-done.6) | copy-start | bytes 98308
  107.7 2.5 %copy-start.9 = (bf16[128,128]{0,1:T(8,128)(2,1)S(1)}, bf16[128,128]{0,1:T(8,128)(2,1)}, u32[]{:S(2)}) copy-start(bf16[128,128]{0,1:T(8,128)(2,1)} %copy-done.8) | copy-start | bytes 98308
  116.1 5.2 %copy-start.11 = (pred[5248]{0:T(1024)(128)(4,1)S(1)}, pred[5248]{0:T(1024)(128)(4,1)}, u32[]{:S(2)}) copy-start(pred[5248]{0:T(1024)(128)(4,1)} %copy-done.10) | copy-start | bytes 15748
  116.1 7.3 %copy-start.1 = (bf16[1,2,640,64]{2,3,1,0:T(8,128)(2,1)S(1)}, bf16[1,2,640,64]{2,3,1,0:T(8,128)(2,1)}, u32[]{:S(2)}) copy-start(bf16[1,2,640,64]{2,3,1,0:T(8,128)(2,1)} %param.12) | copy-start | bytes 491524
where the time goes:
time: 124 us; the launch traced here: 123 us
  starting transfers between devices  30.1 us (24%)
  local copies, waits for them, and re-layouts  29.2 us (24%)
  other arithmetic  19.6 us (16%)
  waiting for transfers between devices  14.3 us (12%)
  blocking collectives  13.6 us (11%)
  matrix products  12.8 us (10%)
  between operations  3.81 us (3%)
    all_to_all x2, starting transfers between devices, exchange_in_order(): filled = lax.all_to_all(filled, axes[k], k, k, tiled=True)  30.1 us
    all_to_all x2, waiting for transfers between devices, exchange_in_order(): filled = lax.all_to_all(filled, axes[k], k, k, tiled=True)  14.3 us
    all_to_all x2, blocking collectives, exchange_in_order(): filled = lax.all_to_all(filled, axes[k], k, k, tiled=True)  13.6 us
    dot_general x1, matrix products, inverse_loop(): lax.dot_general(combined.reshape(field_count * block_count, 2 * wave_coun...  5.96 us
    reshape x1, local copies, waits for them, and re-layouts, inverse_loop(): points = points.reshape(field_count, loop_width)  5.2 us
    another operation x2, other arithmetic  4.37 us
    select_n x1, local copies, waits for them, and re-layouts, forward_loop(): masked = jnp.where(inside[None, :], one_loop, jnp.zeros((), one_loop.dtype))  4.15 us
    select_n x1, other arithmetic, forward_loop(): masked = jnp.where(inside[None, :], one_loop, jnp.zeros((), one_loop.dtype))  3.66 us
  transfers between devices with their start and end apart: 2, of which 2 were waited for; matrix products, arithmetic and copies ran while one was open for 4% of the time, Pallas kernels for 0%

commit v1 on v0

v1 whole, which is shorter than its diff:
```python
import functools
import math

import jax
import jax.numpy as jnp
from jax import lax
from jax.experimental import pallas as pl
from jax.experimental.pallas import tpu as pltpu
from jax.sharding import PartitionSpec as P

TRUNC = 1279
STEP = 0.5
LANES = 128
MESH = pl.DeviceIdType.MESH
HIGHEST = lax.Precision.HIGHEST
F32 = jnp.float32
BF16 = jnp.bfloat16
I32 = jnp.int32

SIN_TERMS = [
    (-1.0) ** k * (2.0 * math.pi) ** (2 * k + 1) / math.factorial(2 * k + 1) for k in range(6)
]


def cos_turn(turn):
    near = turn - jnp.floor(turn + 0.5)
    z = 0.25 - jnp.abs(near)
    z2 = z * z
    total = jnp.full_like(z, SIN_TERMS[-1])
    for term in SIN_TERMS[-2::-1]:
        total = total * z2 + term
    return total * z


def iota(shape, dim):
    return lax.broadcasted_iota(I32, shape, dim)


def dot(a, b, dims=((1,), (0,)), precision=None):
    return lax.dot_general(a, b, (dims, ((), ())), precision=precision, preferred_element_type=F32)


def take_lanes(row8, index):
    return jnp.take_along_axis(row8, index, axis=1, mode="promise_in_bounds")


def for_peers(fn):
    me = lax.axis_index("band")
    x, y, c = me // 16, (me // 2) % 8, me % 2
    cores = [c, (c + 1) % 2]
    ys = [((y + dy) % 8) * 2 for dy in (4, 3, 5, 2, 6, 1, 7, 0)]

    def x_part(k):
        dx = 4 + ((k + 1) // 2) * (1 - 2 * (k % 2))
        return ((x + dx) % 8) * 16

    def most(k, carry):
        base = x_part(k)
        for at, part in enumerate(ys):
            fn(base + part + cores[1])
            if at < 7:
                fn(base + part + cores[0])
        return carry

    def rest(k, carry):
        fn(x_part(k) + ys[7] + cores[0])
        return carry

    lax.fori_loop(0, 8, most, 0)
    lax.fori_loop(0, 7, rest, 0)


def exchange(src, dst, send_sem, recv_sem, own_sem):
    me = lax.axis_index("band")

    def send(peer):
        pltpu.make_async_remote_copy(
            src.at[:, peer],
            dst.at[:, me],
            send_sem,
            recv_sem,
            device_id={"band": peer},
            device_id_type=MESH,
        ).start()

    for_peers(send)
    pltpu.make_async_copy(src.at[:, me], dst.at[:, me], own_sem).start()


def wait_exchange(src, dst, send_sem, recv_sem, own_sem, peers):
    me = lax.axis_index("band")
    some = pl.ds(0, peers)
    pltpu.make_async_copy(src.at[:, me], dst.at[:, me], own_sem).wait()
    pltpu.make_async_copy(src.at[:, some], dst.at[:, some], recv_sem).wait()


def wait_sent(src, dst, send_sem, peers):
    some = pl.ds(0, peers)
    pltpu.make_async_copy(src.at[:, some], dst.at[:, some], send_sem).wait()


def main_kernel(
    grid_hbm,
    leg_hbm,
    gw_hbm,
    vm_hbm,
    cp_hbm,
    mr_hbm,
    ll_hbm,
    lo_hbm,
    wn_hbm,
    a_ref,
    t_ref,
    gbuf,
    leg_v,
    gw_v,
    vm_v,
    cp_v,
    mr_v,
    ll_v,
    lo_v,
    wn_v,
    ll_s,
    lo_s,
    wn_s,
    base_c,
    base_s,
    turn_c,
    turn_s,
    facc,
    send1,
    recv1,
    send2,
    recv2,
    lhs,
    l2t,
    inv,
    kmix,
    vz,
    cz,
    rz,
    vpad,
    gpad,
    wall,
    pf,
    zf,
    loc_sem,
    grid_sem,
    send_sem,
    recv_sem,
    own_sem,
):
    band = lax.axis_index("band")
    fields, width = gbuf.shape
    levels = vm_v.shape[0]
    blocks = width // LANES
    lats = lo_v.shape[1]
    half, rows = leg_v.shape[1:]
    peers = lats - 1
    pairs = 2 * lats
    tiles = send1.shape[0]
    s1 = send1.reshape(tiles, pairs, LANES)
    r1 = recv1.reshape(tiles, pairs, LANES)
    s2 = send2.reshape(tiles, pairs, LANES)
    r2 = recv2.reshape(tiles, pairs, LANES)

    small = [
        (lo_hbm, lo_s),
        (ll_hbm, ll_s),
        (wn_hbm, wn_v),
        (wn_hbm, wn_s),
        (lo_hbm, lo_v),
        (ll_hbm, ll_v),
        (gw_hbm, gw_v),
        (mr_hbm, mr_v),
        (vm_hbm, vm_v),
        (cp_hbm, cp_v),
        (leg_hbm, leg_v),
    ]
    small = [pltpu.make_async_copy(s, d, loc_sem.at[k]) for k, (s, d) in enumerate(small)]
    for copy in small[:3]:
        copy.start()
    chunks = [(k, min(4, blocks - k)) for k in range(0, blocks, 4)]
    loads = []
    for n, (k, count) in enumerate(chunks):
        part = pl.ds(k * LANES, count * LANES)
        loads.append(pltpu.make_async_copy(grid_hbm.at[:, part], gbuf.at[:, part], grid_sem.at[n]))
        loads[-1].start()
    for copy in small[3:]:
        copy.start()

    barrier = pltpu.get_barrier_semaphore()
    for_peers(
        lambda peer: pl.semaphore_signal(
            barrier, inc=1, device_id={"band": peer}, device_id_type=MESH
        )
    )
    facc[fields:, :] = jnp.zeros((facc.shape[0] - fields, pairs), F32)

    for copy in small[:3]:
        copy.wait()
    length = ll_s[0, lo_s[0, band]]
    lane = iota((8, LANES), 1)
    waves8 = jnp.broadcast_to(wn_v[...], (8, LANES))
    waves = jnp.concatenate(
        [take_lanes(waves8, lane // 2 + k * (LANES // 2)) for k in range(2)], axis=1
    )[0:1].astype(F32)
    quarter = (iota((1, pairs), 1) % 2).astype(F32) * 0.25
    length_row = jnp.full((1, pairs), length.astype(F32))
    inv_length = 1.0 / length_row

    def turns(count, stride):
        x = (iota((count, pairs), 0) * stride).astype(F32) * waves
        return (x - jnp.floor(x * inv_length) * length_row) * inv_length

    fine = turns(8, 1) + quarter
    fine_c, fine_s = cos_turn(fine), cos_turn(fine - 0.25)
    mid = turns(16, 8)
    mid_c, mid_s = cos_turn(mid), cos_turn(mid - 0.25)
    for k in range(16):
        c, s = mid_c[k : k + 1], mid_s[k : k + 1]
        base_c[8 * k : 8 * k + 8, :] = c * fine_c - s * fine_s
        base_s[8 * k : 8 * k + 8, :] = s * fine_c + c * fine_s
    far = turns(turn_c.shape[0], LANES)
    turn_c[...] = cos_turn(far)
    turn_s[...] = cos_turn(far - 0.25)
    place = iota((LANES, pairs), 0)
    acc = None
    for n, (k, count) in enumerate(chunks):
        for a in range(k, k + count):
            block = turn_c[a : a + 1, :] * base_c[...] - turn_s[a : a + 1, :] * base_s[...]
            block = jnp.where(place < length - a * LANES, block, 0.0)
            t_ref[a * LANES : (a + 1) * LANES, :] = block.astype(BF16)
        loads[n].wait()
        part = pl.ds(k * LANES, count * LANES)
        product = dot(gbuf[:, part], t_ref[part, :])
        acc = product if acc is None else acc + product
    scale = jnp.where(2.0 * waves < length_row, inv_length, 0.0)
    facc[:fields, :] = acc * scale
    for t in range(tiles):
        s1[t] = facc[t * LANES : (t + 1) * LANES, :].T.astype(BF16)

    pl.semaphore_wait(barrier, peers)
    exchange(send1, recv1, send_sem.at[0], recv_sem.at[0], own_sem.at[0])

    for copy in small[3:]:
        copy.wait()
    wave = wn_s[0, band]
    lat = lo_v[...]
    north = lat < half
    lat_row = jnp.where(north, lat, lats - 1 - lat)
    select = jnp.where(iota((half, lats), 0) == lat_row, 1.0, 0.0)
    sign = jnp.where(north, 1.0, -1.0)
    weight = dot(jnp.broadcast_to(gw_v[...], (8, half)), select, precision=HIGHEST)[0:1]
    select = select.astype(BF16)
    lat8 = jnp.broadcast_to(lat, (8, lats))
    length8 = take_lanes(jnp.broadcast_to(ll_v[...], (8, lats)), lat8)
    length_col = jnp.broadcast_to(length8[0:1].astype(F32), (lats, lats)).T
    lat_col = jnp.broadcast_to(lat.astype(F32), (lats, lats)).T
    north_col = lat_col < half
    sign_col = jnp.where(north_col, 1.0, -1.0)[:, 0:1]
    place_col = jnp.where(north_col, lat_col, lats - 1.0 - lat_col)[:, :half]
    select_t = jnp.where(iota((lats, half), 1).astype(F32) == place_col, 1.0, 0.0).astype(BF16)
    doubling = jnp.where(jnp.full((lats, lats), wave) == 0, 1.0, 2.0)
    wave_f = jnp.full((lats, lats), wave).astype(F32)
    keep_col = jnp.where(2.0 * wave_f < length_col, doubling, 0.0)[:, 0:1]

    rz[...] = jnp.zeros(rz.shape, F32)
    rz[0:1, :levels] = mr_v[...]
    rates = rz[0:1, :]
    for p in range(2):
        table = leg_v[p]
        span = slice(p * rows, (p + 1) * rows)
        degree = iota((rows, LANES), 0) * 2 + (wave + p)
        energy = (degree * (degree + 1)).astype(F32) * (STEP / float(TRUNC * (TRUNC + 1)))
        gain = weight if p == 0 else weight * sign
        own = jnp.where(degree <= TRUNC, dot(table, select, ((0,), (0,))) * gain, 0.0)
        lhs[span, :LANES] = own.astype(BF16)
        lhs[span, LANES:] = (own * -energy).astype(BF16)
        for t in range(2):
            inv[span, t * LANES : (t + 1) * LANES] = 1.0 / (
                1.0 + energy * rates[:, t * LANES : (t + 1) * LANES]
            )
        gain_col = keep_col if p == 0 else keep_col * sign_col
        l2t[:, span] = (dot(select_t, table) * gain_col).astype(BF16)
    mix = dot(l2t[...], lhs[:, :LANES]).astype(BF16)
    spread = []
    for q in range(2):
        each = jnp.where(iota((pairs, lats), 0) == iota((pairs, lats), 1) * 2 + q, 1.0, 0.0)
        each = each.astype(BF16)
        spread.append(dot(dot(each, mix).astype(BF16), each, ((1,), (1,))))
    kmix[...] = (spread[0] + spread[1]).astype(BF16)

    vz[...] = jnp.zeros(vz.shape, F32)
    cz[...] = jnp.zeros(cz.shape, F32)
    vz[:levels, :levels] = vm_v[...]
    cz[:levels, :levels] = cp_v[...]
    modes, couple = vz[...], cz[...]
    square = modes.shape
    vpad[...] = modes.astype(BF16)
    gap = levels - LANES
    shift = jnp.where(iota(square, 0) == iota(square, 1) + gap, 1.0, 0.0)
    moved = dot(shift, couple, ((1,), (1,)), precision=HIGHEST)
    gpad[...] = dot(moved, modes, precision=HIGHEST).astype(BF16)
    wide = (square[0], tiles * LANES)
    shift = jnp.where(iota(wide, 1) == iota(wide, 0) + levels, 1.0, 0.0)
    same = jnp.where(iota(wide, 1) == iota(wide, 0), 1.0, 0.0)
    spread_out = same - STEP * dot(couple, shift, ((0,), (0,)), precision=HIGHEST)
    wall[...] = dot(modes, spread_out, ((0,), (0,)), precision=HIGHEST).astype(BF16)

    wait_exchange(send1, recv1, send_sem.at[0], recv_sem.at[0], own_sem.at[0], peers)
    f0, f1, f2 = r1[0], r1[1], r1[2]
    in_d = dot(jnp.concatenate([f0, f1], axis=1), vpad[...])
    in_p = dot(jnp.concatenate([f1, f2], axis=1), gpad[...])
    for t in range(2):
        pf[t] = in_d[:, t * LANES : (t + 1) * LANES]
        pf[2 + t] = in_p[:, t * LANES : (t + 1) * LANES]
    only_p = jnp.where(iota(f1.shape, 1) < gap, 0.0, 1.0).astype(BF16)
    f1 = f1 * only_p
    own_p = dot(kmix[...], jnp.concatenate([f1, f2], axis=1))
    for q in range(2):
        part = pl.ds(q, lats, stride=2)
        rhs = jnp.concatenate(
            [
                jnp.concatenate([pf[0, part, :], pf[1, part, :]], axis=1),
                jnp.concatenate([pf[2, part, :], pf[3, part, :]], axis=1),
            ],
            axis=0,
        ).astype(BF16)
        total = None
        for k in range(0, 2 * rows, 2 * LANES):
            span = slice(k, k + 2 * LANES)
            solved = (dot(lhs[span, :], rhs) * inv[span, :]).astype(BF16)
            product = dot(l2t[:, span], solved)
            total = product if total is None else total + product
        for t in range(2):
            zf[t, part, :] = total[:, t * LANES : (t + 1) * LANES]
    back = jnp.concatenate([zf[0], zf[1]], axis=1).astype(BF16)
    out = dot(back, wall[...])
    s2[0] = out[:, :LANES].astype(BF16)
    s2[1] = (out[:, LANES : 2 * LANES] + own_p[:, :LANES]).astype(BF16)
    s2[2] = (out[:, 2 * LANES :] + own_p[:, LANES:]).astype(BF16)

    exchange(send2, recv2, send_sem.at[1], recv_sem.at[1], own_sem.at[1])
    wait_sent(send1, recv1, send_sem.at[0], peers)
    wait_exchange(send2, recv2, send_sem.at[1], recv_sem.at[1], own_sem.at[1], peers)
    for t in range(tiles):
        a_ref[t * LANES : (t + 1) * LANES, :] = r2[t].astype(F32).T.astype(BF16)
    wait_sent(send2, recv2, send_sem.at[1], peers)


def inverse_kernel(a_ref, t_ref, out_hbm, obuf, sem):
    fields, width = obuf.shape
    step = 4 * LANES
    copies = []
    for n, k in enumerate(range(0, width, step)):
        part = pl.ds(k, min(step, width - k))
        obuf[:, part] = dot(a_ref[:fields, :], t_ref[part, :], ((1,), (1,))).astype(BF16)
        copies.append(pltpu.make_async_copy(obuf.at[:, part], out_hbm.at[:, part], sem.at[n]))
        copies[-1].start()
    for copy in copies:
        copy.wait()


def per_device(grid_in, legendre, gauss_weight, vertical_modes, coupling, mode_rates, loop_length, lat_order, wave_number):
    fields, width = grid_in.shape[1:]
    rows, half = legendre.shape[2:]
    levels = vertical_modes.shape[0]
    lats = lat_order.shape[0]
    pairs = 2 * lats
    tiles = -(-fields // LANES)
    blocks = width // LANES
    operands = [
        grid_in.reshape(fields, width),
        jnp.swapaxes(legendre.reshape(2, rows, half), 1, 2),
        gauss_weight.reshape(1, half),
        vertical_modes,
        coupling,
        mode_rates.reshape(1, levels),
        loop_length.reshape(1, lats),
        lat_order.reshape(1, lats),
        wave_number.reshape(1, lats),
    ]
    hbm = pl.BlockSpec(memory_space=pltpu.HBM)
    vmem = pl.BlockSpec(memory_space=pltpu.VMEM)
    dma = pltpu.SemaphoreType.DMA
    a_mat, table = pl.pallas_call(
        main_kernel,
        out_shape=(
            pltpu.VMEM((tiles * LANES, pairs), BF16),
            pltpu.VMEM((width, pairs), BF16),
        ),
        in_specs=[hbm] * 9,
        out_specs=(vmem, vmem),
        scratch_shapes=[
            pltpu.VMEM((fields, width), BF16),
            pltpu.VMEM((2, half, rows), BF16),
            pltpu.VMEM((1, half), F32),
            pltpu.VMEM((levels, levels), F32),
            pltpu.VMEM((levels, levels), F32),
            pltpu.VMEM((1, levels), F32),
            pltpu.VMEM((1, lats), I32),
            pltpu.VMEM((1, lats), I32),
            pltpu.VMEM((1, lats), I32),
            pltpu.SMEM((1, lats), I32),
            pltpu.SMEM((1, lats), I32),
            pltpu.SMEM((1, lats), I32),
            pltpu.VMEM((LANES, pairs), F32),
            pltpu.VMEM((LANES, pairs), F32),
            pltpu.VMEM((-(-blocks // 8) * 8, pairs), F32),
            pltpu.VMEM((-(-blocks // 8) * 8, pairs), F32),
            pltpu.VMEM((tiles * LANES, pairs), F32),
            pltpu.VMEM((tiles, lats, 2, LANES), BF16),
            pltpu.VMEM((tiles, lats, 2, LANES), BF16),
            pltpu.VMEM((tiles, lats, 2, LANES), BF16),
            pltpu.VMEM((tiles, lats, 2, LANES), BF16),
            pltpu.VMEM((2 * rows, 2 * LANES), BF16),
            pltpu.VMEM((lats, 2 * rows), BF16),
            pltpu.VMEM((2 * rows, 2 * LANES), F32),
            pltpu.VMEM((pairs, pairs), BF16),
            pltpu.VMEM((2 * LANES, 2 * LANES), F32),
            pltpu.VMEM((2 * LANES, 2 * LANES), F32),
            pltpu.VMEM((8, 2 * LANES), F32),
            pltpu.VMEM((2 * LANES, 2 * LANES), BF16),
            pltpu.VMEM((2 * LANES, 2 * LANES), BF16),
            pltpu.VMEM((2 * LANES, tiles * LANES), BF16),
            pltpu.VMEM((4, pairs, LANES), F32),
            pltpu.VMEM((2, pairs, LANES), F32),
            dma((11,)),
            dma((-(-blocks // 4),)),
            dma((2,)),
            dma((2,)),
            dma((2,)),
        ],
        compiler_params=pltpu.CompilerParams(
            collective_id=1, has_side_effects=True, vmem_limit_bytes=40 * 2**20
        ),
        name="spectral_step",
    )(*[pltpu.with_memory_space_constraint(each, pltpu.HBM) for each in operands])
    a_mat = pltpu.with_memory_space_constraint(a_mat, pltpu.VMEM)
    table = pltpu.with_memory_space_constraint(table, pltpu.VMEM)
    points = pl.pallas_call(
        inverse_kernel,
        out_shape=jax.ShapeDtypeStruct((fields, width), BF16),
        in_specs=[vmem, vmem],
        out_specs=hbm,
        scratch_shapes=[pltpu.VMEM((fields, width), BF16), dma((-(-blocks // 4),))],
        compiler_params=pltpu.CompilerParams(vmem_limit_bytes=16 * 2**20),
        name="inverse_loop",
    )(a_mat, table)
    return points.reshape(grid_in.shape)


def solution(mesh):
    whole = P(("member", "band"), None, None)
    in_specs = (whole, P("band", None, None, None)) + (P(),) * 7
    return jax.shard_map(per_device, mesh=mesh, in_specs=in_specs, out_specs=whole, check_vma=False)
```

time: 124 us -> 47 us (0.38)
  Pallas kernels: 0 us -> 46.9 us
  starting transfers between devices: 30.1 us -> 0 us
  local copies, waits for them, and re-layouts: 29.2 us -> 0 us
  other arithmetic: 19.6 us -> 0 us
  waiting for transfers between devices: 14.3 us -> 0 us
  blocking collectives: 13.6 us -> 0 us
  matrix products: 12.8 us -> 0 us
  between operations: 3.81 us -> 0.01 us
    pallas_call x0 -> x2, Pallas kernels: none -> 46.9 us  [the longest x1 44.9 us: per_device(): pl.pallas_call(main_kernel, out_shape=(pltpu.VMEM((tiles * LANES, pairs),...]
    all_to_all x2 -> x0, starting transfers between devices: 30.1 us -> none  [exchange_in_order(): filled = lax.all_to_all(filled, axes[k], k, k, tiled=True)]
    all_to_all x2 -> x0, waiting for transfers between devices: 14.3 us -> none  [exchange_in_order(): filled = lax.all_to_all(filled, axes[k], k, k, tiled=True)]
    all_to_all x2 -> x0, blocking collectives: 13.6 us -> none  [exchange_in_order(): filled = lax.all_to_all(filled, axes[k], k, k, tiled=True)]
    dot_general x7 -> x0, matrix products: 12.8 us -> none  [the longest x1 5.96 us: inverse_loop(): lax.dot_general(combined.reshape(field_count * block_count, 2 * wave_coun...]
    reshape x3 -> x0, local copies, waits for them, and re-layouts: 6.08 us -> none  [the longest x1 5.2 us: inverse_loop(): points = points.reshape(field_count, loop_width)]
    select_n x3 -> x0, local copies, waits for them, and re-layouts: 5.62 us -> none  [the longest x1 4.15 us: forward_loop(): masked = jnp.where(inside[None, :], one_loop, jnp.zeros((), one_loop.dtype))]
    another operation x4 -> x0, other arithmetic: 4.66 us -> none
  transfers between devices with their start and end apart: 2 -> 0, of which waited for: 2 -> 0; matrix products, arithmetic and copies ran while one was open for 4% -> 0% of each run, Pallas kernels for 0% -> 0%
where the time goes in v1:
time: 47 us; the launch traced here: 46.9 us
  Pallas kernels  46.9 us (100%)
    pallas_call x1, Pallas kernels, per_device(): pl.pallas_call(main_kernel, out_shape=(pltpu.VMEM((tiles * LANES, pairs),...  44.9 us
    pallas_call x1, Pallas kernels, per_device(): pl.pallas_call(inverse_kernel, out_shape=jax.ShapeDtypeStruct((fields, wi...  1.94 us

profile of v1, /device:TPU:513, one launch (start us, length us, event | category | flops | bytes accessed | tf_op | source)
XLA Modules:
  0.0 46.9 jit_solution(10448003609060737459)
XLA Ops:
  0.0 44.9 %spectral_step.1 = (bf16[384,256]{1,0:T(8,128)(2,1)S(1)}, bf16[5248,256]{1,0:T(8,128)(2,1)S(1)}) custom-call(bf16[274,5248]{1,0:T(8,128)(2,1)} %bitcast.10, bf16[2,64,640]{2,1,0:T(8,128)(2,1)} %bitcast.11, f32[1,64]{1,0:T(1,128)} %bitcast.13, f32[137,137]{1,0:T(8,128)} %vm_hbm.1, f32[137,137]{1,0:T(8,128)} %cp_hbm.1, f32[1,137]{1,0:T(1,128)} %bitcast.12, ...), custom_call_target="tpu_custom_call" | custom-call | tf_op jit(solution)/shard_map/spectral_step/pallas_call | solution.py:387
  44.9 1.9 %inverse_loop.1 = bf16[274,5248]{1,0:T(8,128)(2,1)} custom-call(bf16[384,256]{1,0:T(8,128)(2,1)S(1)} %get-tuple-element.7.a_ref, bf16[5248,256]{1,0:T(8,128)(2,1)S(1)} %get-tuple-element.8.t_ref), custom_call_target="tpu_custom_call" | custom-call | tf_op jit(solution)/shard_map/inverse_loop/pallas_call | solution.py:442

commit v2 on v1

--- a/solution.py
+++ b/solution.py
@@ -44,34 +44,50 @@
     return jnp.take_along_axis(row8, index, axis=1, mode="promise_in_bounds")
 
 
-def for_peers(fn):
+FAR_FIRST = (4, 3, 5, 2, 6, 1, 7, 0)
+
+
+def far_first(k):
+    return 4 + ((k + 1) // 2) * (1 - 2 * (k % 2))
+
+
+def place():
     me = lax.axis_index("band")
-    x, y, c = me // 16, (me // 2) % 8, me % 2
-    cores = [c, (c + 1) % 2]
-    ys = [((y + dy) % 8) * 2 for dy in (4, 3, 5, 2, 6, 1, 7, 0)]
-
-    def x_part(k):
-        dx = 4 + ((k + 1) // 2) * (1 - 2 * (k % 2))
-        return ((x + dx) % 8) * 16
-
-    def most(k, carry):
-        base = x_part(k)
-        for at, part in enumerate(ys):
-            fn(base + part + cores[1])
-            if at < 7:
-                fn(base + part + cores[0])
-        return carry
-
-    def rest(k, carry):
-        fn(x_part(k) + ys[7] + cores[0])
-        return carry
-
-    lax.fori_loop(0, 8, most, 0)
-    lax.fori_loop(0, 7, rest, 0)
-
-
-def exchange(src, dst, send_sem, recv_sem, own_sem):
+    return me // 16, (me // 2) % 8, me % 2
+
+
+def at_place(x, y, c):
+    return (x % 8) * 16 + (y % 8) * 2 + c % 2
+
+
+def signal(sem, peer):
+    pl.semaphore_signal(sem, inc=1, device_id={"band": peer}, device_id_type=MESH)
+
+
+def greet(barrier):
+    x, y, c = place()
+    for dx in FAR_FIRST:
+        for dc in (1, 0):
+            if dx or dc:
+                signal(barrier, at_place(x + dx, y, c + dc))
+    for dy in FAR_FIRST[:7]:
+        signal(barrier, at_place(x, y + dy, c))
+
+
+GREETINGS = 22
+
+
+def announce(ready):
+    x, y, c = place()
+    for k, dy in enumerate(FAR_FIRST[:7]):
+        signal(ready.at[FAR_FIRST.index((8 - dy) % 8)], at_place(x, y + dy, c))
+
+
+def exchange(src, dst, send_sem, recv_sem, own_sem, ready=None):
     me = lax.axis_index("band")
+    x, y, c = place()
+    parts = [((x + dx) % 8) * 16 for dx in FAR_FIRST]
+    cores = [(c + 1) % 2, c]
 
     def send(peer):
         pltpu.make_async_remote_copy(
@@ -83,7 +99,19 @@
             device_id_type=MESH,
         ).start()
 
-    for_peers(send)
+    def column(k, carry):
+        if ready is not None:
+            pl.semaphore_wait(ready.at[k], 1)
+        base = ((y + far_first(k)) % 8) * 2
+        for part in parts:
+            for core in cores:
+                send(base + part + core)
+        return carry
+
+    lax.fori_loop(0, 7, column, 0)
+    for n, part in enumerate(parts):
+        for core in cores[: 2 if n < 7 else 1]:
+            send(y * 2 + part + core)
     pltpu.make_async_copy(src.at[:, me], dst.at[:, me], own_sem).start()
 
 
@@ -149,6 +177,7 @@
     send_sem,
     recv_sem,
     own_sem,
+    ready,
 ):
     band = lax.axis_index("band")
     fields, width = gbuf.shape
@@ -190,11 +219,7 @@
         copy.start()
 
     barrier = pltpu.get_barrier_semaphore()
-    for_peers(
-        lambda peer: pl.semaphore_signal(
-            barrier, inc=1, device_id={"band": peer}, device_id_type=MESH
-        )
-    )
+    greet(barrier)
     facc[fields:, :] = jnp.zeros((facc.shape[0] - fields, pairs), F32)
 
     for copy in small[:3]:
@@ -224,12 +249,12 @@
     far = turns(turn_c.shape[0], LANES)
     turn_c[...] = cos_turn(far)
     turn_s[...] = cos_turn(far - 0.25)
-    place = iota((LANES, pairs), 0)
+    within = iota((LANES, pairs), 0)
     acc = None
     for n, (k, count) in enumerate(chunks):
         for a in range(k, k + count):
             block = turn_c[a : a + 1, :] * base_c[...] - turn_s[a : a + 1, :] * base_s[...]
-            block = jnp.where(place < length - a * LANES, block, 0.0)
+            block = jnp.where(within < length - a * LANES, block, 0.0)
             t_ref[a * LANES : (a + 1) * LANES, :] = block.astype(BF16)
         loads[n].wait()
         part = pl.ds(k * LANES, count * LANES)
@@ -240,8 +265,9 @@
     for t in range(tiles):
         s1[t] = facc[t * LANES : (t + 1) * LANES, :].T.astype(BF16)
 
-    pl.semaphore_wait(barrier, peers)
-    exchange(send1, recv1, send_sem.at[0], recv_sem.at[0], own_sem.at[0])
+    pl.semaphore_wait(barrier, GREETINGS)
+    announce(ready)
+    exchange(send1, recv1, send_sem.at[0], recv_sem.at[0], own_sem.at[0], ready)
 
     for copy in small[3:]:
         copy.wait()
@@ -431,6 +457,7 @@
             dma((2,)),
             dma((2,)),
             dma((2,)),
+            pltpu.SemaphoreType.REGULAR((7,)),
         ],
         compiler_params=pltpu.CompilerParams(
             collective_id=1, has_side_effects=True, vmem_limit_bytes=40 * 2**20

time: 47 us -> 46.2 us (0.983)
  Pallas kernels: 46.9 us -> 46 us
    pallas_call x1, Pallas kernels: 44.9 us -> 44.1 us  [per_device(): pl.pallas_call(main_kernel, out_shape=(pltpu.VMEM((tiles * LANES, pairs),...]
where the time goes in v2:
time: 46.2 us; the launch traced here: 46.1 us
  Pallas kernels  46 us (100%)
    pallas_call x1, Pallas kernels, per_device(): pl.pallas_call(main_kernel, out_shape=(pltpu.VMEM((tiles * LANES, pairs),...  44.1 us
    pallas_call x1, Pallas kernels, per_device(): pl.pallas_call(inverse_kernel, out_shape=jax.ShapeDtypeStruct((fields, wi...  1.94 us

profile of v2, /device:TPU:513, one launch (start us, length us, event | category | flops | bytes accessed | tf_op | source)
XLA Modules:
  0.0 46.1 jit_solution(16113070506711405793)
XLA Ops:
  0.0 44.1 %spectral_step.1 = (bf16[384,256]{1,0:T(8,128)(2,1)S(1)}, bf16[5248,256]{1,0:T(8,128)(2,1)S(1)}) custom-call(bf16[274,5248]{1,0:T(8,128)(2,1)} %bitcast.10, bf16[2,64,640]{2,1,0:T(8,128)(2,1)} %bitcast.11, f32[1,64]{1,0:T(1,128)} %bitcast.13, f32[137,137]{1,0:T(8,128)} %vm_hbm.1, f32[137,137]{1,0:T(8,128)} %cp_hbm.1, f32[1,137]{1,0:T(1,128)} %bitcast.12, ...), custom_call_target="tpu_custom_call" | custom-call | tf_op jit(solution)/shard_map/spectral_step/pallas_call | solution.py:413
  44.1 1.9 %inverse_loop.1 = bf16[274,5248]{1,0:T(8,128)(2,1)} custom-call(bf16[384,256]{1,0:T(8,128)(2,1)S(1)} %get-tuple-element.7.a_ref, bf16[5248,256]{1,0:T(8,128)(2,1)S(1)} %get-tuple-element.8.t_ref), custom_call_target="tpu_custom_call" | custom-call | tf_op jit(solution)/shard_map/inverse_loop/pallas_call | solution.py:469

commit v3 on v2

--- a/solution.py
+++ b/solution.py
@@ -172,6 +172,7 @@
     wall,
     pf,
     zf,
+    solved,
     loc_sem,
     grid_sem,
     send_sem,
@@ -193,6 +194,8 @@
     s2 = send2.reshape(tiles, pairs, LANES)
     r2 = recv2.reshape(tiles, pairs, LANES)
 
+    barrier = pltpu.get_barrier_semaphore()
+    greet(barrier)
     small = [
         (lo_hbm, lo_s),
         (ll_hbm, ll_s),
@@ -218,8 +221,6 @@
     for copy in small[3:]:
         copy.start()
 
-    barrier = pltpu.get_barrier_semaphore()
-    greet(barrier)
     facc[fields:, :] = jnp.zeros((facc.shape[0] - fields, pairs), F32)
 
     for copy in small[:3]:
@@ -336,35 +337,39 @@
 
     wait_exchange(send1, recv1, send_sem.at[0], recv_sem.at[0], own_sem.at[0], peers)
     f0, f1, f2 = r1[0], r1[1], r1[2]
+    last = jnp.concatenate([f1, f2], axis=1)
     in_d = dot(jnp.concatenate([f0, f1], axis=1), vpad[...])
-    in_p = dot(jnp.concatenate([f1, f2], axis=1), gpad[...])
+    in_p = dot(last, gpad[...])
     for t in range(2):
         pf[t] = in_d[:, t * LANES : (t + 1) * LANES]
         pf[2 + t] = in_p[:, t * LANES : (t + 1) * LANES]
-    only_p = jnp.where(iota(f1.shape, 1) < gap, 0.0, 1.0).astype(BF16)
-    f1 = f1 * only_p
-    own_p = dot(kmix[...], jnp.concatenate([f1, f2], axis=1))
-    for q in range(2):
-        part = pl.ds(q, lats, stride=2)
-        rhs = jnp.concatenate(
-            [
-                jnp.concatenate([pf[0, part, :], pf[1, part, :]], axis=1),
-                jnp.concatenate([pf[2, part, :], pf[3, part, :]], axis=1),
-            ],
-            axis=0,
-        ).astype(BF16)
-        total = None
-        for k in range(0, 2 * rows, 2 * LANES):
-            span = slice(k, k + 2 * LANES)
-            solved = (dot(lhs[span, :], rhs) * inv[span, :]).astype(BF16)
-            product = dot(l2t[:, span], solved)
-            total = product if total is None else total + product
+
+    parts = [pl.ds(q, lats, stride=2) for q in range(2)]
+    rhs = []
+    for part in parts:
+        both = [jnp.concatenate([pf[n, part, :], pf[n + 1, part, :]], axis=1) for n in (0, 2)]
+        rhs.append(jnp.concatenate(both, axis=0).astype(BF16))
+
+    wide_rhs = jnp.concatenate(rhs, axis=1)
+    own_p = dot(kmix[...], last)
+    for k in range(0, 2 * rows, 256):
+        span = slice(k, k + 256)
+        each = dot(lhs[span, :], wide_rhs)
+        share = inv[span, :]
+        for q in range(2):
+            half_q = slice(2 * q * LANES, 2 * (q + 1) * LANES)
+            solved[span, half_q] = (each[:, half_q] * share).astype(BF16)
+    both = dot(l2t[...], solved[...])
+    totals = [both[:, : 2 * LANES], both[:, 2 * LANES :]]
+    for q, part in enumerate(parts):
         for t in range(2):
-            zf[t, part, :] = total[:, t * LANES : (t + 1) * LANES]
+            zf[t, part, :] = totals[q][:, t * LANES : (t + 1) * LANES]
+
     back = jnp.concatenate([zf[0], zf[1]], axis=1).astype(BF16)
     out = dot(back, wall[...])
+    only_p = iota((pairs, LANES), 1) >= gap
     s2[0] = out[:, :LANES].astype(BF16)
-    s2[1] = (out[:, LANES : 2 * LANES] + own_p[:, :LANES]).astype(BF16)
+    s2[1] = (out[:, LANES : 2 * LANES] + jnp.where(only_p, own_p[:, :LANES], 0.0)).astype(BF16)
     s2[2] = (out[:, 2 * LANES :] + own_p[:, LANES:]).astype(BF16)
 
     exchange(send2, recv2, send_sem.at[1], recv_sem.at[1], own_sem.at[1])
@@ -452,6 +457,7 @@
             pltpu.VMEM((2 * LANES, tiles * LANES), BF16),
             pltpu.VMEM((4, pairs, LANES), F32),
             pltpu.VMEM((2, pairs, LANES), F32),
+            pltpu.VMEM((2 * rows, 4 * LANES), BF16),
             dma((11,)),
             dma((-(-blocks // 4),)),
             dma((2,)),

time: 46.2 us -> 45.6 us (0.987)
  Pallas kernels: 46 us -> 45.5 us
    pallas_call x1, Pallas kernels: 44.1 us -> 43.6 us  [per_device(): pl.pallas_call(main_kernel, out_shape=(pltpu.VMEM((tiles * LANES, pairs),...]
where the time goes in v3:
time: 45.6 us; the launch traced here: 45.5 us
  Pallas kernels  45.5 us (100%)
    pallas_call x1, Pallas kernels, per_device(): pl.pallas_call(main_kernel, out_shape=(pltpu.VMEM((tiles * LANES, pairs),...  43.6 us
    pallas_call x1, Pallas kernels, per_device(): pl.pallas_call(inverse_kernel, out_shape=jax.ShapeDtypeStruct((fields, wi...  1.94 us

profile of v3, /device:TPU:513, one launch (start us, length us, event | category | flops | bytes accessed | tf_op | source)
XLA Modules:
  0.0 45.5 jit_solution(10937367529341001849)
XLA Ops:
  0.0 43.6 %spectral_step.1 = (bf16[384,256]{1,0:T(8,128)(2,1)S(1)}, bf16[5248,256]{1,0:T(8,128)(2,1)S(1)}) custom-call(bf16[274,5248]{1,0:T(8,128)(2,1)} %bitcast.10, bf16[2,64,640]{2,1,0:T(8,128)(2,1)} %bitcast.11, f32[1,64]{1,0:T(1,128)} %bitcast.13, f32[137,137]{1,0:T(8,128)} %vm_hbm.1, f32[137,137]{1,0:T(8,128)} %cp_hbm.1, f32[1,137]{1,0:T(1,128)} %bitcast.12, ...), custom_call_target="tpu_custom_call" | custom-call | tf_op jit(solution)/shard_map/spectral_step/pallas_call | solution.py:418
  43.6 1.9 %inverse_loop.1 = bf16[274,5248]{1,0:T(8,128)(2,1)} custom-call(bf16[384,256]{1,0:T(8,128)(2,1)S(1)} %get-tuple-element.7.a_ref, bf16[5248,256]{1,0:T(8,128)(2,1)S(1)} %get-tuple-element.8.t_ref), custom_call_target="tpu_custom_call" | custom-call | tf_op jit(solution)/shard_map/inverse_loop/pallas_call | solution.py:475

commit v4 on v3

--- a/solution.py
+++ b/solution.py
@@ -66,12 +66,12 @@
 
 def greet(barrier):
     x, y, c = place()
-    for dx in FAR_FIRST:
+    for dy in FAR_FIRST:
         for dc in (1, 0):
-            if dx or dc:
-                signal(barrier, at_place(x + dx, y, c + dc))
-    for dy in FAR_FIRST[:7]:
-        signal(barrier, at_place(x, y + dy, c))
+            if dy or dc:
+                signal(barrier, at_place(x, y + dy, c + dc))
+    for dx in FAR_FIRST[:7]:
+        signal(barrier, at_place(x + dx, y, c))
 
 
 GREETINGS = 22
@@ -79,14 +79,15 @@
 
 def announce(ready):
     x, y, c = place()
-    for k, dy in enumerate(FAR_FIRST[:7]):
-        signal(ready.at[FAR_FIRST.index((8 - dy) % 8)], at_place(x, y + dy, c))
+    for dx in FAR_FIRST[:7]:
+        signal(ready.at[FAR_FIRST.index((8 - dx) % 8)], at_place(x + dx, y, c))
 
 
 def exchange(src, dst, send_sem, recv_sem, own_sem, ready=None):
     me = lax.axis_index("band")
     x, y, c = place()
-    parts = [((x + dx) % 8) * 16 for dx in FAR_FIRST]
+    outer, inner = ((x, 16), (y, 2)) if ready is not None else ((y, 2), (x, 16))
+    parts = [((inner[0] + d) % 8) * inner[1] for d in FAR_FIRST]
     cores = [(c + 1) % 2, c]
 
     def send(peer):
@@ -99,19 +100,19 @@
             device_id_type=MESH,
         ).start()
 
-    def column(k, carry):
+    def line(k, carry):
         if ready is not None:
             pl.semaphore_wait(ready.at[k], 1)
-        base = ((y + far_first(k)) % 8) * 2
+        base = ((outer[0] + far_first(k)) % 8) * outer[1]
         for part in parts:
             for core in cores:
                 send(base + part + core)
         return carry
 
-    lax.fori_loop(0, 7, column, 0)
+    lax.fori_loop(0, 7, line, 0)
     for n, part in enumerate(parts):
         for core in cores[: 2 if n < 7 else 1]:
-            send(y * 2 + part + core)
+            send(outer[0] * outer[1] + part + core)
     pltpu.make_async_copy(src.at[:, me], dst.at[:, me], own_sem).start()
 
 
@@ -250,24 +251,32 @@
     far = turns(turn_c.shape[0], LANES)
     turn_c[...] = cos_turn(far)
     turn_s[...] = cos_turn(far - 0.25)
-    within = iota((LANES, pairs), 0)
-    acc = None
+    group = 16
+    within = iota((group, pairs), 0)
+    middle = -(-fields // 32) * 16
+    split = [slice(0, middle), slice(middle, fields)]
+    acc = [None, None]
     for n, (k, count) in enumerate(chunks):
-        for a in range(k, k + count):
-            block = turn_c[a : a + 1, :] * base_c[...] - turn_s[a : a + 1, :] * base_s[...]
-            block = jnp.where(within < length - a * LANES, block, 0.0)
-            t_ref[a * LANES : (a + 1) * LANES, :] = block.astype(BF16)
+        for g in range(0, LANES, group):
+            base = base_c[g : g + group, :], base_s[g : g + group, :]
+            for a in range(k, k + count):
+                block = turn_c[a : a + 1, :] * base[0] - turn_s[a : a + 1, :] * base[1]
+                block = jnp.where(within < length - (a * LANES + g), block, 0.0)
+                t_ref[a * LANES + g : a * LANES + g + group, :] = block.astype(BF16)
         loads[n].wait()
         part = pl.ds(k * LANES, count * LANES)
-        product = dot(gbuf[:, part], t_ref[part, :])
-        acc = product if acc is None else acc + product
+        for m, some in enumerate(split):
+            product = dot(gbuf[some, part], t_ref[part, :])
+            acc[m] = product if n == 0 else acc[m] + product
+        if n == len(chunks) // 2 - 1:
+            pl.semaphore_wait(barrier, GREETINGS)
+            announce(ready)
     scale = jnp.where(2.0 * waves < length_row, inv_length, 0.0)
-    facc[:fields, :] = acc * scale
+    for some, total in zip(split, acc):
+        facc[some, :] = total * scale
     for t in range(tiles):
         s1[t] = facc[t * LANES : (t + 1) * LANES, :].T.astype(BF16)
 
-    pl.semaphore_wait(barrier, GREETINGS)
-    announce(ready)
     exchange(send1, recv1, send_sem.at[0], recv_sem.at[0], own_sem.at[0], ready)
 
     for copy in small[3:]:

time: 45.6 us -> 44.3 us (0.971)
  Pallas kernels: 45.5 us -> 44.1 us
    pallas_call x1, Pallas kernels: 43.6 us -> 42.2 us  [per_device(): pl.pallas_call(main_kernel, out_shape=(pltpu.VMEM((tiles * LANES, pairs),...]
where the time goes in v4:
time: 44.3 us; the launch traced here: 44.2 us
  Pallas kernels  44.1 us (100%)
    pallas_call x1, Pallas kernels, per_device(): pl.pallas_call(main_kernel, out_shape=(pltpu.VMEM((tiles * LANES, pairs),...  42.2 us
    pallas_call x1, Pallas kernels, per_device(): pl.pallas_call(inverse_kernel, out_shape=jax.ShapeDtypeStruct((fields, wi...  1.94 us

profile of v4, /device:TPU:513, one launch (start us, length us, event | category | flops | bytes accessed | tf_op | source)
XLA Modules:
  0.0 44.2 jit_solution(6521213282375802471)
XLA Ops:
  0.0 42.2 %spectral_step.1 = (bf16[384,256]{1,0:T(8,128)(2,1)S(1)}, bf16[5248,256]{1,0:T(8,128)(2,1)S(1)}) custom-call(bf16[274,5248]{1,0:T(8,128)(2,1)} %bitcast.10, bf16[2,64,640]{2,1,0:T(8,128)(2,1)} %bitcast.11, f32[1,64]{1,0:T(1,128)} %bitcast.13, f32[137,137]{1,0:T(8,128)} %vm_hbm.1, f32[137,137]{1,0:T(8,128)} %cp_hbm.1, f32[1,137]{1,0:T(1,128)} %bitcast.12, ...), custom_call_target="tpu_custom_call" | custom-call | tf_op jit(solution)/shard_map/spectral_step/pallas_call | solution.py:427
  42.2 1.9 %inverse_loop.1 = bf16[274,5248]{1,0:T(8,128)(2,1)} custom-call(bf16[384,256]{1,0:T(8,128)(2,1)S(1)} %get-tuple-element.7.a_ref, bf16[5248,256]{1,0:T(8,128)(2,1)S(1)} %get-tuple-element.8.t_ref), custom_call_target="tpu_custom_call" | custom-call | tf_op jit(solution)/shard_map/inverse_loop/pallas_call | solution.py:484

commit v5 on v4

--- a/solution.py
+++ b/solution.py
@@ -109,10 +109,16 @@
                 send(base + part + core)
         return carry
 
+    def own_line():
+        for n, part in enumerate(parts):
+            for core in cores[: 2 if n < 7 else 1]:
+                send(outer[0] * outer[1] + part + core)
+
+    if ready is not None:
+        own_line()
     lax.fori_loop(0, 7, line, 0)
-    for n, part in enumerate(parts):
-        for core in cores[: 2 if n < 7 else 1]:
-            send(outer[0] * outer[1] + part + core)
+    if ready is None:
+        own_line()
     pltpu.make_async_copy(src.at[:, me], dst.at[:, me], own_sem).start()
 
 
@@ -268,7 +274,7 @@
         for m, some in enumerate(split):
             product = dot(gbuf[some, part], t_ref[part, :])
             acc[m] = product if n == 0 else acc[m] + product
-        if n == len(chunks) // 2 - 1:
+        if n == 1:
             pl.semaphore_wait(barrier, GREETINGS)
             announce(ready)
     scale = jnp.where(2.0 * waves < length_row, inv_length, 0.0)
@@ -385,7 +391,7 @@
     wait_sent(send1, recv1, send_sem.at[0], peers)
     wait_exchange(send2, recv2, send_sem.at[1], recv_sem.at[1], own_sem.at[1], peers)
     for t in range(tiles):
-        a_ref[t * LANES : (t + 1) * LANES, :] = r2[t].astype(F32).T.astype(BF16)
+        a_ref[t * LANES : (t + 1) * LANES, :] = r2[t].T
     wait_sent(send2, recv2, send_sem.at[1], peers)
 
 

time: 44.3 us -> 44.1 us (level)
  no operation moved by 1% of the time
where the time goes in v5:
time: 44.1 us; the launch traced here: 44 us
  Pallas kernels  44 us (100%)
    pallas_call x1, Pallas kernels, per_device(): pl.pallas_call(main_kernel, out_shape=(pltpu.VMEM((tiles * LANES, pairs),...  42.1 us
    pallas_call x1, Pallas kernels, per_device(): pl.pallas_call(inverse_kernel, out_shape=jax.ShapeDtypeStruct((fields, wi...  1.94 us

profile of v5, /device:TPU:513, one launch (start us, length us, event | category | flops | bytes accessed | tf_op | source)
XLA Modules:
  0.0 44.0 jit_solution(15696390932914984777)
XLA Ops:
  0.0 42.1 %spectral_step.1 = (bf16[384,256]{1,0:T(8,128)(2,1)S(1)}, bf16[5248,256]{1,0:T(8,128)(2,1)S(1)}) custom-call(bf16[274,5248]{1,0:T(8,128)(2,1)} %bitcast.10, bf16[2,64,640]{2,1,0:T(8,128)(2,1)} %bitcast.11, f32[1,64]{1,0:T(1,128)} %bitcast.13, f32[137,137]{1,0:T(8,128)} %vm_hbm.1, f32[137,137]{1,0:T(8,128)} %cp_hbm.1, f32[1,137]{1,0:T(1,128)} %bitcast.12, ...), custom_call_target="tpu_custom_call" | custom-call | tf_op jit(solution)/shard_map/spectral_step/pallas_call | solution.py:433
  42.1 1.9 %inverse_loop.1 = bf16[274,5248]{1,0:T(8,128)(2,1)} custom-call(bf16[384,256]{1,0:T(8,128)(2,1)S(1)} %get-tuple-element.7.a_ref, bf16[5248,256]{1,0:T(8,128)(2,1)S(1)} %get-tuple-element.8.t_ref), custom_call_target="tpu_custom_call" | custom-call | tf_op jit(solution)/shard_map/inverse_loop/pallas_call | solution.py:490
